TPU v7x, 32 devices: a whole 2x2x4 slice. The times are simulated.
32 devices in a mesh: member: 4 (over y, core), space: 8 (over z, x).
Axes of the slice: x: 2, y: 2, z: 4, core: 2. Of those that a mesh axis runs over, the one named last changes fastest.
Arguments:
- state: float32 [256, 128, 1024], P('member', 'space'), may hold values from -8 to 8
- obs_index: int32 [8192], P('space'), may hold values from 0 to 16383
- obs_value: float32 [8192], P('space'), may hold values from -6 to 6
- obs_scale: float32 [8192], P('space'), may hold values from 0.3 to 3
- ksat: float32 [128, 1024], P('space'), may hold values from 0.05 to 0.2
- storage: float32 [128, 1024], P('space'), may hold values from 0.5 to 4
- recharge: float32 [128, 1024], P('space'), may hold values from -1.8 to 1.8
- newton_counts: int32 [256], replicated, may hold values from 1 to 8, as said below
Outputs:
- forecast: float32 [256, 128, 1024], P('member', 'space')
Inputs may be any that keep to these rules, and one draw needn't show every extreme that they name: `newton_counts`: A count of 8 occurs in every draw.
All inputs are finite; a program needn't handle non-finite values.
Results may differ from a plain program's by a relative error of at most 0.0003.
Values sent between devices are 32-bit elements; how exact they have to be, the bound alone decides.
A program may use at most 64 MiB of HBM per device.

v0:
```python
import jax
import jax.numpy as jnp
from jax import lax
from jax.sharding import PartitionSpec as P

KMAX = 8
NS_ITERS = 12
HIGHEST_PRECISION = lax.Precision.HIGHEST
DAMPING = 0.3


def padded_2(array, sides, width):
    for axis, dim in sides:
        peers, length = (lax.axis_size(axis), array.shape[dim])
        up = [(i, (i + 1) % peers) for i in range(peers - 1)]
        down = [(j, i) for i, j in up]
        last = lax.slice_in_dim(array, length - width, length, axis=dim)
        leading = lax.slice_in_dim(array, 0, width, axis=dim)
        before = lax.ppermute(last, axis, up)
        after = lax.ppermute(leading, axis, down)
        array = jnp.concatenate([before, array, after], axis=dim)
    return array


def inverse_root(gram_matrix):
    order_size = gram_matrix.shape[0]
    identity = jnp.eye(order_size, dtype=jnp.float32)
    whole = identity + gram_matrix
    norm_value = jnp.sqrt(jnp.sum(whole * whole))
    upper_iter = whole / norm_value
    lower_iter = identity
    for sweep_index in range(NS_ITERS):
        middle = 1.5 * identity - 0.5 * jnp.dot(lower_iter, upper_iter, precision=HIGHEST_PRECISION)
        upper_iter = jnp.dot(upper_iter, middle, precision=HIGHEST_PRECISION)
        lower_iter = jnp.dot(middle, lower_iter, precision=HIGHEST_PRECISION)
    return lower_iter / jnp.sqrt(norm_value)


def face_flux(padded, conduct):
    wide_level = jnp.pad(padded, ((0, 0), (0, 0), (1, 1)))
    wide_cond = jnp.pad(conduct, ((0, 0), (0, 0), (1, 1)))
    centre_level = wide_level[:, 1:-1, 1:-1]
    centre_cond = wide_cond[:, 1:-1, 1:-1]
    height = centre_level.shape[1]
    breadth = centre_level.shape[2]
    divergence = jnp.zeros_like(centre_level)
    for offset_row, offset_col in ((0, 1), (2, 1), (1, 0), (1, 2)):
        other_level = wide_level[
            :, offset_row : offset_row + height, offset_col : offset_col + breadth
        ]
        other_cond = wide_cond[
            :, offset_row : offset_row + height, offset_col : offset_col + breadth
        ]
        divergence = divergence + 0.5 * (centre_cond + other_cond) * (other_level - centre_level)
    return divergence


def sweep_group(start_iter, goal, storage, group_counts):

    def sweep_once(sweep_index, iterate):
        bend_value = jnp.tanh(iterate)
        derivative = 1.0 + storage * (1.0 - bend_value * bend_value)
        stepped = iterate - DAMPING * (iterate + storage * bend_value - goal) / derivative
        return jnp.where((group_counts > sweep_index)[:, None, None], stepped, iterate)

    return lax.fori_loop(0, jnp.max(group_counts), sweep_once, start_iter)


def relax(pressure, drive_term, storage, counts):
    target = pressure + storage * jnp.tanh(pressure) + drive_term
    pieces = []
    for first_member in range(0, pressure.shape[0], 8):
        pieces.append(
            sweep_group(
                pressure[first_member : first_member + 8],
                target[first_member : first_member + 8],
                storage,
                counts[first_member : first_member + 8],
            )
        )
    return jnp.concatenate(pieces, axis=0)


def advance(padded, padded_ksat, storage, recharge, counts):
    conduct = padded_ksat * jax.nn.sigmoid(padded)
    drive_term = face_flux(padded, conduct) + recharge
    return relax(padded[:, 1:-1], drive_term, storage, counts)


def on_device(state, obs_index, obs_value, obs_scale, ksat, storage, recharge, newton_counts):
    local_members, tile_rows, tile_width = state.shape
    groups = lax.axis_size("member")
    members = local_members * groups
    tile_cells = tile_rows * tile_width
    block_cells = tile_cells // groups
    share = local_members // groups
    position = lax.axis_index("member")
    regrouped = lax.all_to_all(
        state.reshape(local_members, tile_cells), "member", split_axis=1, concat_axis=0, tiled=True
    )
    mean_state = jnp.mean(regrouped, axis=0)
    anomaly = regrouped - mean_state
    local_cell = obs_index - position * block_cells
    inside = (local_cell >= 0) & (local_cell < block_cells)
    picked = jnp.clip(local_cell, 0, block_cells - 1)
    weight = jnp.where(inside, obs_scale, 0.0)
    root_count = jnp.sqrt(jnp.float32(members - 1))
    spread = jnp.take(anomaly, picked, axis=1) * weight / root_count
    innovation = weight * (obs_value - jnp.take(mean_state, picked))
    gram_part = jnp.dot(spread, spread.T, precision=HIGHEST_PRECISION)
    drive_part = jnp.dot(spread, innovation, precision=HIGHEST_PRECISION)
    gram_matrix, drive_vector = lax.psum((gram_part, drive_part), ("member", "space"))
    root_inverse = inverse_root(gram_matrix)
    mean_weights = jnp.dot(
        root_inverse,
        jnp.dot(root_inverse, drive_vector, precision=HIGHEST_PRECISION),
        precision=HIGHEST_PRECISION,
    )
    transform = mean_weights[:, None] / root_count + root_inverse
    sequence = jnp.arange(members, dtype=jnp.int32)
    owner_of = sequence // local_members
    sort_key = owner_of * ((KMAX + 1) * members) + (KMAX - newton_counts) * members + sequence
    ranking = jnp.argsort(sort_key)
    member_ids = ranking.reshape(groups, share, groups).transpose(2, 0, 1).reshape(members)
    transform = jnp.take(transform, member_ids, axis=1)
    own_ids = lax.dynamic_slice_in_dim(member_ids, position * local_members, local_members)
    own_counts = jnp.take(newton_counts, own_ids)
    analysis = mean_state + jnp.dot(transform.T, anomaly, precision=HIGHEST_PRECISION)
    owned = lax.all_to_all(analysis, "member", split_axis=0, concat_axis=1, tiled=True)
    pressure = owned.reshape(local_members, tile_rows, tile_width)
    stacked = jnp.concatenate([pressure, ksat[None]], axis=0)
    widened = padded_2(stacked, (("space", 1),), 1)
    ksat_wide = widened[local_members]
    pressure = advance(widened[:local_members], ksat_wide, storage, recharge, own_counts)
    widened = padded_2(pressure, (("space", 1),), 1)
    pressure = advance(widened, ksat_wide, storage, recharge, own_counts)
    final_field = pressure.reshape(local_members, tile_cells)
    arrived = lax.all_to_all(final_field, "member", split_axis=0, concat_axis=0, tiled=True)
    by_owner = member_ids.reshape(groups, groups, share)
    arrived_ids = (
        jnp.take(by_owner, position, axis=1).reshape(local_members) - position * local_members
    )
    final_field = jnp.take(arrived, jnp.argsort(arrived_ids), axis=0)
    return final_field.reshape(local_members, tile_rows, tile_width)


def solution(mesh):
    return jax.shard_map(
        on_device,
        mesh=mesh,
        in_specs=(
            P("member", "space", None),
            P("space"),
            P("space"),
            P("space"),
            P("space", None),
            P("space", None),
            P("space", None),
            P(),
        ),
        out_specs=P("member", "space", None),
        check_vma=False,
    )
```

profile of v0, /device:TPU:8, one launch (start us, length us, event | category | flops | bytes accessed | tf_op | source)
XLA Modules:
  0.0 656.5 jit_solution(13870586919959672134)
XLA Ops:
  6.5 5.8 all_to_all.34
  12.4 6.6 %copy.22 = f32[64,4,4096]{2,0,1:T(8,128)} copy(f32[64,4,4096]{2,1,0:T(4,128)} %all_to_all.34) | data formatting | bytes 8388608 | tf_op jit(solution)/shard_map/all_to_all | solution.py:98
  19.0 5.0 all-to-all-start
  24.0 3.2 sort.34
  27.6 44.5 %all-to-all-done = f32[64,4,4096]{2,0,1:T(8,128)} async-done(((f32[64,4,4096]{2,0,1:T(8,128)}), f32[64,4,4096]{2,0,1:T(8,128)}, u32[]{:S(2)}, u32[]{:S(2)}) %all-to-all-start) | async-done | bytes 4194336 | tf_op jit(solution)/shard_map/all_to_all | solution.py:98
  72.1 2.4 reduce_sum.18
  74.6 6.2 gather_fusion.1
  80.7 4.8 bitcast_subtract_fusion
  85.5 5.6 copy.24
  91.1 5.7 gather_fusion
  96.9 3.1 fusion.40
  100.8 39.6 %psum.15 = f32[256]{0:T(256)S(1)} all-reduce(f32[256]{0:T(256)S(1)} %bitcast.112), channel_id=1, replica_groups=mesh['member'=4,'space'=8] {'member','space'}, use_global_device_ids=true, to_apply=%region_5.6 | all-reduce | flops 256 | bytes 2048 | tf_op jit(solution)/shard_map/psum | solution.py:112
  140.4 86.6 %all-reduce.6.cloned.1.call-done = f32[256,256]{1,0:T(8,128)} async-done(((f32[256,256]{1,0:T(8,128)}), f32[256,256]{1,0:T(8,128)}) %all-reduce.6.cloned.1.call-update) | async-done | bytes 262160 | tf_op jit(solution)/shard_map/psum | solution.py:112
  247.0 8.2 %convolution_add_fusion = f32[256,4096]{1,0:T(8,128)} fusion(f32[256,4096]{1,0:T(8,128)} %bitcast_subtract_fusion, f32[4096]{0:T(1024)S(1)} %broadcast_multiply_fusion, f32[256,256]{1,0:T(8,128)S(1)} %gather_fusion.2, pred[256]{0:T(512)(128)(4,1)S(1)} %compare_and_fusion.1), kind=kOutput, calls=%fused_computation.51 | convolution fusion | flops 3222339584 | bytes 8667392 | tf_op jit(solution)/shard_map/dot_general | solution.py:128
  255.2 4.8 all-to-all-start.1
  262.5 45.8 %all-to-all-done.1 = f32[4,64,4096]{2,1,0:T(8,128)} async-done(((f32[4,64,4096]{2,1,0:T(8,128)}), f32[4,64,4096]{2,1,0:T(8,128)}, u32[]{:S(2)}, u32[]{:S(2)}) %all-to-all-start.1) | async-done | bytes 4194336 | tf_op jit(solution)/shard_map/all_to_all | solution.py:129
  308.3 6.9 %copy.28 = f32[64,4,4096]{2,1,0:T(4,128)} copy(f32[64,4,4096]{2,0,1:T(8,128)} %bitcast.13) | data formatting | bytes 8388608 | tf_op jit(solution)/shard_map/all_to_all | solution.py:129
  315.2 5.8 reshape.171
  321.0 3.6 pad_maximum_fusion.11
  324.6 3.4 collective-permute-start
  328.0 3.5 collective-permute-start.1
  331.5 3.3 fusion.69
  359.2 3.8 pad_maximum_fusion
  363.1 15.7 %fusion.6 = f32[64,16,1024]{2,1,0:T(8,128)} fusion(f32[64,18,1024]{2,1,0:T(8,128)S(1)} %get-tuple-element.768, f32[64,16,1024]{2,1,0:T(8,128)S(1)} %copy-done.2, f32[64,18,1024]{2,1,0:T(8,128)S(1)} %get-tuple-element.767, f32[65,1,1024]{2,1,0:T(1,128)} %collective-permute-done.1, f32[1,16,1024]{2,1,0:T(8,128)S(1)} %bitcast.106, ...), kind=kLoop, calls=%fused_computation.58 | loop fusion | flops 28311552 | bytes 34283520 | tf_op jit(solution)/shard_map/add | solution.py:70
  378.8 4.1 fusion.68
  382.9 6.3 while.168
  383.5 2.3 subtract_select_fusion.39
  386.4 2.3 subtract_select_fusion.39
  389.3 9.4 %while.167 = (s32[]{:T(128)}, f32[8,16,1024]{2,1,0:T(8,128)}, s32[]{:T(128)}, s32[8]{0:T(128)S(1)}, f32[16,1024]{1,0:T(8,128)S(1)}, /*index=5*/f32[8,16,1024]{2,1,0:T(8,128)}, s32[]{:T(128)}) while((s32[]{:T(128)}, f32[8,16,1024]{2,1,0:T(8,128)}, s32[]{:T(128)}, s32[8]{0:T(128)S(1)}, f32[16,1024]{1,0:T(8,128)S(1)}, ...), condition=%wide.region_26.27_spmd, body=%wide.region_25.26_spmd.sunk | while | flops 1441802 | bytes 1638537 | solution.py:66
  389.9 2.2 subtract_select_fusion.38
  392.8 2.2 subtract_select_fusion.38
  395.8 2.2 subtract_select_fusion.38
  398.7 4.9 while.166
  403.6 6.9 %while.165 = (s32[]{:T(128)}, f32[8,16,1024]{2,1,0:T(8,128)S(1)}, s32[]{:T(128)}, s32[8]{0:T(128)S(1)}, f32[16,1024]{1,0:T(8,128)S(1)}, /*index=5*/f32[8,16,1024]{2,1,0:T(8,128)}, s32[]{:T(128)}) while((s32[]{:T(128)}, f32[8,16,1024]{2,1,0:T(8,128)S(1)}, s32[]{:T(128)}, s32[8]{0:T(128)S(1)}, f32[16,1024]{1,0:T(8,128)S(1)}, ...), condition=%wide.region_20.21_spmd, body=%wide.region_19.20_spmd.sunk | while | flops 1441802 | bytes 1638537 | solution.py:66
  410.5 7.2 %while.164 = (s32[]{:T(128)}, f32[8,16,1024]{2,1,0:T(8,128)S(1)}, s32[]{:T(128)}, s32[8]{0:T(128)S(1)}, f32[16,1024]{1,0:T(8,128)S(1)}, /*index=5*/f32[8,16,1024]{2,1,0:T(8,128)}, s32[]{:T(128)}) while((s32[]{:T(128)}, f32[8,16,1024]{2,1,0:T(8,128)S(1)}, s32[]{:T(128)}, s32[8]{0:T(128)S(1)}, f32[16,1024]{1,0:T(8,128)S(1)}, ...), condition=%wide.region_17.18_spmd, body=%wide.region_16.17_spmd.sunk | while | flops 1441802 | bytes 1638537 | solution.py:66
  417.7 16.9 %while.163 = (s32[]{:T(128)}, f32[8,16,1024]{2,1,0:T(8,128)S(1)}, s32[]{:T(128)}, s32[8]{0:T(128)S(1)}, f32[16,1024]{1,0:T(8,128)S(1)}, /*index=5*/f32[8,16,1024]{2,1,0:T(8,128)}, s32[]{:T(128)}) while((s32[]{:T(128)}, f32[8,16,1024]{2,1,0:T(8,128)S(1)}, s32[]{:T(128)}, s32[8]{0:T(128)S(1)}, f32[16,1024]{1,0:T(8,128)S(1)}, ...), condition=%wide.region_14.15_spmd, body=%wide.region_13.14_spmd.sunk | while | flops 1441802 | bytes 1638537 | solution.py:66
  434.6 4.6 while.162
  439.1 17.4 %while.161 = (s32[]{:T(128)}, f32[8,16,1024]{2,1,0:T(8,128)S(1)}, s32[]{:T(128)}, s32[8]{0:T(128)S(1)}, f32[16,1024]{1,0:T(8,128)S(1)}, /*index=5*/f32[8,16,1024]{2,1,0:T(8,128)}, s32[]{:T(128)}) while((s32[]{:T(128)}, f32[8,16,1024]{2,1,0:T(8,128)S(1)}, s32[]{:T(128)}, s32[8]{0:T(128)S(1)}, f32[16,1024]{1,0:T(8,128)S(1)}, ...), condition=%wide.region_8.9_spmd, body=%wide.region_7.8_spmd.sunk | while | flops 1441802 | bytes 1638537 | solution.py:66
  461.1 2.5 collective-permute-start.2
  463.6 4.3 collective-permute-start.3
  467.9 6.3 collective-permute-done.2
  474.2 2.8 collective-permute-done.3
  477.0 3.8 pad_maximum_fusion.3
  480.9 11.3 %fusion.18 = f32[64,16,1024]{2,1,0:T(8,128)} fusion(f32[64,18,1024]{2,1,0:T(8,128)S(1)} %get-tuple-element.770, f32[64,16,1024]{2,1,0:T(8,128)S(1)} %copy-done.8, f32[64,18,1024]{2,1,0:T(8,128)S(1)} %get-tuple-element.769, f32[64,1,1024]{2,1,0:T(1,128)} %collective-permute-done.3, f32[64,1,1024]{2,1,0:T(1,128)S(1)} %collective-permute-done.2, ...), kind=kLoop, calls=%fused_computation.70 | loop fusion | flops 26214400 | bytes 34209792 | tf_op jit(solution)/shard_map/add | solution.py:70
  492.2 4.1 fusion.66
  496.3 6.3 while.176
  496.9 2.3 subtract_select_fusion.47
  499.8 2.3 subtract_select_fusion.47
  502.7 9.4 %while.175 = (s32[]{:T(128)}, f32[8,16,1024]{2,1,0:T(8,128)}, s32[]{:T(128)}, s32[8]{0:T(128)S(1)}, f32[16,1024]{1,0:T(8,128)S(1)}, /*index=5*/f32[8,16,1024]{2,1,0:T(8,128)}, s32[]{:T(128)}) while((s32[]{:T(128)}, f32[8,16,1024]{2,1,0:T(8,128)}, s32[]{:T(128)}, s32[8]{0:T(128)S(1)}, f32[16,1024]{1,0:T(8,128)S(1)}, ...), condition=%wide.region_43.44_spmd, body=%wide.region_42.43_spmd.sunk | while | flops 1441802 | bytes 1638537 | solution.py:66
  503.3 2.2 subtract_select_fusion.46
  506.2 2.2 subtract_select_fusion.46
  509.1 2.2 subtract_select_fusion.46
  512.0 4.9 while.174
  517.0 6.6 %while.173 = (s32[]{:T(128)}, f32[8,16,1024]{2,1,0:T(8,128)S(1)}, s32[]{:T(128)}, s32[8]{0:T(128)S(1)}, f32[16,1024]{1,0:T(8,128)S(1)}, /*index=5*/f32[8,16,1024]{2,1,0:T(8,128)}, s32[]{:T(128)}) while((s32[]{:T(128)}, f32[8,16,1024]{2,1,0:T(8,128)S(1)}, s32[]{:T(128)}, s32[8]{0:T(128)S(1)}, f32[16,1024]{1,0:T(8,128)S(1)}, ...), condition=%wide.region_39.40_spmd, body=%wide.region_38.39_spmd.sunk | while | flops 1441802 | bytes 1638537 | solution.py:66
  523.6 7.2 %while.172 = (s32[]{:T(128)}, f32[8,16,1024]{2,1,0:T(8,128)S(1)}, s32[]{:T(128)}, s32[8]{0:T(128)S(1)}, f32[16,1024]{1,0:T(8,128)S(1)}, /*index=5*/f32[8,16,1024]{2,1,0:T(8,128)}, s32[]{:T(128)}) while((s32[]{:T(128)}, f32[8,16,1024]{2,1,0:T(8,128)S(1)}, s32[]{:T(128)}, s32[8]{0:T(128)S(1)}, f32[16,1024]{1,0:T(8,128)S(1)}, ...), condition=%wide.region_37.38_spmd, body=%wide.region_36.37_spmd.sunk | while | flops 1441802 | bytes 1638537 | solution.py:66
  530.8 16.9 %while.171 = (s32[]{:T(128)}, f32[8,16,1024]{2,1,0:T(8,128)S(1)}, s32[]{:T(128)}, s32[8]{0:T(128)S(1)}, f32[16,1024]{1,0:T(8,128)S(1)}, /*index=5*/f32[8,16,1024]{2,1,0:T(8,128)}, s32[]{:T(128)}) while((s32[]{:T(128)}, f32[8,16,1024]{2,1,0:T(8,128)S(1)}, s32[]{:T(128)}, s32[8]{0:T(128)S(1)}, f32[16,1024]{1,0:T(8,128)S(1)}, ...), condition=%wide.region_35.36_spmd, body=%wide.region_34.35_spmd.sunk | while | flops 1441802 | bytes 1638537 | solution.py:66
  547.7 4.6 while.170
  552.3 17.4 %while.169 = (s32[]{:T(128)}, f32[8,16,1024]{2,1,0:T(8,128)S(1)}, s32[]{:T(128)}, s32[8]{0:T(128)S(1)}, f32[16,1024]{1,0:T(8,128)S(1)}, /*index=5*/f32[8,16,1024]{2,1,0:T(8,128)}, s32[]{:T(128)}) while((s32[]{:T(128)}, f32[8,16,1024]{2,1,0:T(8,128)S(1)}, s32[]{:T(128)}, s32[8]{0:T(128)S(1)}, f32[16,1024]{1,0:T(8,128)S(1)}, ...), condition=%wide.region_31.32_spmd, body=%wide.region_30.31_spmd.sunk | while | flops 1441802 | bytes 1638537 | solution.py:66
  576.3 5.0 all_to_all.41
  581.3 5.1 all-to-all-start.2
  589.3 45.2 %all-to-all-done.2 = f32[4,16,16384]{2,1,0:T(8,128)} async-done(((f32[4,16,16384]{2,1,0:T(8,128)}), f32[4,16,16384]{2,1,0:T(8,128)}, u32[]{:S(2)}, u32[]{:S(2)}) %all-to-all-start.2) | async-done | bytes 4194336 | tf_op jit(solution)/shard_map/all_to_all | solution.py:138
  634.6 7.7 %gather_fusion.4 = f32[64,16384]{1,0:T(8,128)} fusion(f32[64,16384]{1,0:T(8,128)} %bitcast.16, s32[1024]{0:T(1024)S(1)} %pad_clamp_fusion), kind=kCustom, calls=%fused_computation.4 | custom fusion | bytes 8388864 | tf_op jit(solution)/shard_map/jit(_take)/gather | solution.py:143
  642.3 4.6 copy.36
  646.8 2.4 bitcast_select_fusion
  (263 shorter events, 136.0 us)
Async XLA Ops:
  19.0 5.0 copy-start.1
  19.0 8.6 %copy-start.14 = (s32[1024]{0:T(1024)S(1)}, s32[1024]{0:T(1024)}, u32[]{:S(2)}) copy-start(s32[1024]{0:T(1024)} %param.41) | copy-start | bytes 12292
  19.0 53.2 %all-to-all-start = ((f32[64,4,4096]{2,0,1:T(8,128)}), f32[64,4,4096]{2,0,1:T(8,128)}, u32[]{:S(2)}, u32[]{:S(2)}) async-start(f32[64,4,4096]{2,0,1:T(8,128)} %copy.22), calls=%async_computation | async-start | bytes 8388608 | tf_op jit(solution)/shard_map/all_to_all | solution.py:98
  23.9 203.0 %all-reduce.6.cloned.1.call-start = ((), (), s32[]{:S(2)}) async-start(), calls=%async_computation.3 | async-start | bytes 524288 | tf_op jit(solution)/shard_map/psum | solution.py:112
  27.3 44.8 %copy-start.13 = (s32[4,16,4]{2,1,0:T(8,128)}, s32[4,16,4]{2,1,0:T(8,128)S(1)}, u32[]{:S(2)}) copy-start(s32[4,16,4]{2,1,0:T(8,128)S(1)} %reshape.168) | copy-start | bytes 3076
  91.1 5.7 copy-start.15
  91.1 5.7 copy-start.16
  255.2 53.0 %all-to-all-start.1 = ((f32[4,64,4096]{2,1,0:T(8,128)}), f32[4,64,4096]{2,1,0:T(8,128)}, u32[]{:S(2)}, u32[]{:S(2)}) async-start(f32[4,64,4096]{2,1,0:T(8,128)} %bitcast.102), calls=%async_computation.1 | async-start | bytes 8388608 | tf_op jit(solution)/shard_map/all_to_all | solution.py:129
  315.2 5.8 copy-start.9
  324.6 32.5 %collective-permute-start = (f32[65,1,1024]{2,1,0:T(1,128)}, f32[65,1,1024]{2,1,0:T(1,128)S(1)}, u32[]{:S(2)}, u32[]{:S(2)}) collective-permute-start(f32[65,1,1024]{2,1,0:T(1,128)} %get-tuple-element.771), channel_id=1, source_target_pairs={{0,1},{1,2},{2,3},{3,4},{4,5},{5,6},{6,7},{8,9},{9,10},{10,11},{11... | collective-permute-start | bytes 798728 | tf_op jit(solution)/shard_map/ppermute | solution.py:19
  328.0 29.1 %collective-permute-start.1 = (f32[65,1,1024]{2,1,0:T(1,128)}, f32[65,1,1024]{2,1,0:T(1,128)}, u32[]{:S(2)}, u32[]{:S(2)}) collective-permute-start(f32[65,1,1024]{2,1,0:T(1,128)} %get-tuple-element.772), channel_id=1, source_target_pairs={{1,0},{2,1},{3,2},{4,3},{5,4},{6,5},{7,6},{9,8},{10,9},{11,10},{12... | collective-permute-start | bytes 798728 | tf_op jit(solution)/shard_map/ppermute | solution.py:20
  357.0 2.2 copy-start.2
  359.2 3.8 copy-start.10
  359.2 3.8 copy-start
  359.2 3.8 copy-start.11
  378.8 4.1 copy-start.21
  382.9 6.4 copy-start.20
  389.2 9.4 %copy-start.19 = (s32[8]{0:T(128)S(1)}, s32[8]{0:T(128)}, u32[]{:S(2)}) copy-start(s32[8]{0:T(128)} %get-tuple-element.1693) | copy-start | bytes 100
  398.6 5.0 copy-start.18
  403.6 6.9 %copy-start.17 = (s32[8]{0:T(128)S(1)}, s32[8]{0:T(128)}, u32[]{:S(2)}) copy-start(s32[8]{0:T(128)} %get-tuple-element.1651) | copy-start | bytes 100
  456.5 1.0 copy-start.3
  456.6 1.2 copy-start.5
  457.8 2.0 copy-start.7
  461.1 13.1 %collective-permute-start.2 = (f32[64,1,1024]{2,1,0:T(1,128)}, f32[64,1,1024]{2,1,0:T(1,128)S(1)}, u32[]{:S(2)}, u32[]{:S(2)}) collective-permute-start(f32[64,1,1024]{2,1,0:T(1,128)} %get-tuple-element.781), channel_id=1, source_target_pairs={{0,1},{1,2},{2,3},{3,4},{4,5},{5,6},{6,7},{8,9},{9,10},{10,11},{11... | collective-permute-start | bytes 786440 | tf_op jit(solution)/shard_map/ppermute | solution.py:19
  463.6 13.4 %collective-permute-start.3 = (f32[64,1,1024]{2,1,0:T(1,128)}, f32[64,1,1024]{2,1,0:T(1,128)}, u32[]{:S(2)}, u32[]{:S(2)}) collective-permute-start(f32[64,1,1024]{2,1,0:T(1,128)} %get-tuple-element.782), channel_id=1, source_target_pairs={{1,0},{2,1},{3,2},{4,3},{5,4},{6,5},{7,6},{9,8},{10,9},{11,10},{12... | collective-permute-start | bytes 786440 | tf_op jit(solution)/shard_map/ppermute | solution.py:20
  467.9 13.0 %copy-start.8 = (f32[64,16,1024]{2,1,0:T(8,128)S(1)}, f32[64,16,1024]{2,1,0:T(8,128)}, u32[]{:S(2)}) copy-start(f32[64,16,1024]{2,1,0:T(8,128)} %copy-done.7) | copy-start | bytes 12582916
  467.9 13.0 %copy-start.12 = (f32[16,1024]{1,0:T(8,128)S(1)}, f32[16,1024]{1,0:T(8,128)}, u32[]{:S(2)}) copy-start(f32[16,1024]{1,0:T(8,128)} %param.46) | copy-start | bytes 196612
  569.7 5.0 copy-start.4
  569.7 5.8 copy-start.6
  581.3 53.3 %all-to-all-start.2 = ((f32[4,16,16384]{2,1,0:T(8,128)}), f32[4,16,16384]{2,1,0:T(8,128)}, u32[]{:S(2)}, u32[]{:S(2)}) async-start(f32[4,16,16384]{2,1,0:T(8,128)} %all_to_all.41), calls=%async_computation.2 | async-start | bytes 8388608 | tf_op jit(solution)/shard_map/all_to_all | solution.py:138
Sparse Core Ops, SparseCore 0:
  100.1 126.7 all-reduce.5
where the time goes:
time: 669 us; the launch traced here: 656 us
  waiting for transfers between devices  231 us (35%)
  other arithmetic  155 us (23%)
  local copies, waits for them, and re-layouts  109 us (16%)
  loops' own time  49.4 us (7%)
  blocking collectives  39.6 us (6%)
  starting transfers between devices  28.5 us (4%)
  matrix products  28.2 us (4%)
  between operations  15.5 us (2%)
    select_n x62, other arithmetic, sweep_once(): jnp.where((group_counts > sweep_index)[:, None, None], stepped, iterate)  97 us
    psum x1, waiting for transfers between devices, on_device(): lax.psum((gram_part, drive_part), ('member', 'space'))  86.6 us
    another operation x16, loops' own time, sweep_group(): return lax.fori_loop(0, jnp.max(group_counts), sweep_once, start_iter)  49.4 us
    all_to_all x1, waiting for transfers between devices, on_device(): lax.all_to_all(analysis, 'member', split_axis=0, concat_axis=1, tiled=True)  45.8 us
    all_to_all x1, waiting for transfers between devices, on_device(): lax.all_to_all(final_field, 'member', split_axis=0, concat_axis=0, tiled=...  45.2 us
    all_to_all x1, waiting for transfers between devices, on_device(): lax.all_to_all(state.reshape(local_members, tile_cells), 'member', split_...  44.5 us
    psum x1, blocking collectives, on_device(): lax.psum((gram_part, drive_part), ('member', 'space'))  39.6 us
    add x2, other arithmetic, relax(): target = pressure + storage * jnp.tanh(pressure) + drive_term  27 us
  transfers between devices with their start and end apart: 8, of which 6 were waited for; matrix products, arithmetic and copies ran while one was open for 5% of the time, Pallas kernels for 0%

commit v1 on v0

--- a/solution.py
+++ b/solution.py
@@ -126,7 +126,10 @@
     own_ids = lax.dynamic_slice_in_dim(member_ids, position * local_members, local_members)
     own_counts = jnp.take(newton_counts, own_ids)
     analysis = mean_state + jnp.dot(transform.T, anomaly, precision=HIGHEST_PRECISION)
-    owned = lax.all_to_all(analysis, "member", split_axis=0, concat_axis=1, tiled=True)
+    size = lax.axis_size("member")
+    blocks = jnp.stack(jnp.split(analysis, size, axis=0), axis=0)
+    blocks = lax.all_to_all(blocks, "member", split_axis=0, concat_axis=0)
+    owned = jnp.concatenate(blocks, axis=1)
     pressure = owned.reshape(local_members, tile_rows, tile_width)
     stacked = jnp.concatenate([pressure, ksat[None]], axis=0)
     widened = padded_2(stacked, (("space", 1),), 1)

time: 669 us -> 667 us (level)
    all_to_all x1 -> x0, local copies, waits for them, and re-layouts: 6.9 us -> none  [on_device(): lax.all_to_all(analysis, 'member', split_axis=0, concat_axis=1, tiled=True)]
    unnamed x59 -> x73, local copies, waits for them, and re-layouts: 14.9 us -> 15.1 us
where the time goes in v1:
time: 667 us; the launch traced here: 655 us
  waiting for transfers between devices  231 us (35%)
  other arithmetic  159 us (24%)
  local copies, waits for them, and re-layouts  105 us (16%)
  loops' own time  50.2 us (8%)
  blocking collectives  39.6 us (6%)
  starting transfers between devices  28.6 us (4%)
  matrix products  25.4 us (4%)
  between operations  15.6 us (2%)
    select_n x62, other arithmetic, sweep_once(): jnp.where((group_counts > sweep_index)[:, None, None], stepped, iterate)  97.1 us
    psum x1, waiting for transfers between devices, on_device(): lax.psum((gram_part, drive_part), ('member', 'space'))  86.6 us
    another operation x16, loops' own time, sweep_group(): return lax.fori_loop(0, jnp.max(group_counts), sweep_once, start_iter)  50.2 us
    all_to_all x1, waiting for transfers between devices, on_device(): blocks = lax.all_to_all(blocks, 'member', split_axis=0, concat_axis=0)  45.7 us
    all_to_all x1, waiting for transfers between devices, on_device(): lax.all_to_all(final_field, 'member', split_axis=0, concat_axis=0, tiled=...  45.2 us
    all_to_all x1, waiting for transfers between devices, on_device(): lax.all_to_all(state.reshape(local_members, tile_cells), 'member', split_...  44.5 us
    psum x1, blocking collectives, on_device(): lax.psum((gram_part, drive_part), ('member', 'space'))  39.6 us
    slice x17, local copies, waits for them, and re-layouts, relax(): pressure[first_member:first_member + 8]  25.6 us
  transfers between devices with their start and end apart: 8, of which 6 were waited for; matrix products, arithmetic and copies ran while one was open for 5% of the time, Pallas kernels for 0%

profile of v1, /device:TPU:8, one launch (start us, length us, event | category | flops | bytes accessed | tf_op | source)
XLA Modules:
  0.0 654.6 jit_solution(14161417522981812840)
XLA Ops:
  6.5 5.8 all_to_all.25
  12.4 6.6 %copy.13 = f32[64,4,4096]{2,0,1:T(8,128)} copy(f32[64,4,4096]{2,1,0:T(4,128)} %all_to_all.25) | data formatting | bytes 8388608 | tf_op jit(solution)/shard_map/all_to_all | solution.py:98
  19.0 5.0 all-to-all-start
  24.0 3.2 sort.34
  27.7 44.5 %all-to-all-done = f32[64,4,4096]{2,0,1:T(8,128)} async-done(((f32[64,4,4096]{2,0,1:T(8,128)}), f32[64,4,4096]{2,0,1:T(8,128)}, u32[]{:S(2)}, u32[]{:S(2)}) %all-to-all-start) | async-done | bytes 4194336 | tf_op jit(solution)/shard_map/all_to_all | solution.py:98
  72.2 2.4 reduce_sum.18
  74.6 6.2 gather_fusion.1
  80.7 4.8 bitcast_subtract_fusion
  85.5 5.6 copy.15
  91.2 5.7 gather_fusion
  96.9 3.1 fusion.40
  100.8 39.6 %psum.15 = f32[256]{0:T(256)S(1)} all-reduce(f32[256]{0:T(256)S(1)} %bitcast.118), channel_id=1, replica_groups=mesh['member'=4,'space'=8] {'member','space'}, use_global_device_ids=true, to_apply=%region_5.6 | all-reduce | flops 256 | bytes 2048 | tf_op jit(solution)/shard_map/psum | solution.py:112
  140.4 86.6 %all-reduce.6.cloned.1.call-done = f32[256,256]{1,0:T(8,128)} async-done(((f32[256,256]{1,0:T(8,128)}), f32[256,256]{1,0:T(8,128)}) %all-reduce.6.cloned.1.call-update) | async-done | bytes 262160 | tf_op jit(solution)/shard_map/psum | solution.py:112
  247.0 5.5 convolution_add_fusion
  252.8 2.4 pad_maximum_fusion.10
  255.2 4.9 all-to-all-start.1
  262.6 45.7 %all-to-all-done.1 = f32[4,64,4096]{2,1,0:T(8,128)} async-done(((f32[4,64,4096]{2,1,0:T(8,128)}), f32[4,64,4096]{2,1,0:T(8,128)}, u32[]{:S(2)}, u32[]{:S(2)}) %all-to-all-start.1) | async-done | bytes 4194336 | tf_op jit(solution)/shard_map/all_to_all | solution.py:131
  308.3 6.9 %copy.19 = f32[64,4,4096]{2,1,0:T(4,128)} copy(f32[64,4,4096]{2,0,1:T(8,128)} %bitcast.16) | data formatting | bytes 8388608 | tf_op jit(solution)/shard_map/reshape | solution.py:132
  315.2 5.9 reshape_reshape.3
  321.1 3.5 pad_maximum_fusion.12
  324.6 3.4 collective-permute-start
  328.0 3.5 collective-permute-start.1
  331.5 3.4 fusion.69
  338.2 2.2 copy.25
  359.5 3.8 pad_maximum_fusion
  363.3 15.0 %fusion.6 = f32[64,16,1024]{2,1,0:T(8,128)S(1)} fusion(f32[64,18,1024]{2,1,0:T(8,128)S(1)} %get-tuple-element.768, f32[64,16,1024]{2,1,0:T(8,128)S(1)} %copy-done.2, f32[64,18,1024]{2,1,0:T(8,128)S(1)} %get-tuple-element.767, f32[65,1,1024]{2,1,0:T(1,128)} %collective-permute-done.1, f32[1,16,1024]{2,1,0:T(8,128)} %bitcast.109, f32[65,1,1024]{2,1,0:T(1,128)} %copy-done.9, ...), kind=kLoop, calls=%fused_computation.58 | loop fusion | flops 28311552 | bytes 34283520 | tf_op jit(solution)/shard_map/add | solution.py:70
  380.3 7.5 %while.168 = (s32[]{:T(128)}, f32[8,16,1024]{2,1,0:T(8,128)}, s32[]{:T(128)}, s32[8]{0:T(128)}, f32[16,1024]{1,0:T(8,128)S(1)}, /*index=5*/f32[8,16,1024]{2,1,0:T(8,128)}, s32[]{:T(128)}) while((s32[]{:T(128)}, f32[8,16,1024]{2,1,0:T(8,128)}, s32[]{:T(128)}, s32[8]{0:T(128)}, f32[16,1024]{1,0:T(8,128)S(1)}, ...), condition=%wide.region_29.30_spmd, body=%wide.region_28.29_spmd.sunk | while | flops 1441802 | bytes 1638537 | solution.py:66
  381.5 2.3 subtract_select_fusion.39
  385.0 2.3 subtract_select_fusion.39
  387.9 9.4 %while.167 = (s32[]{:T(128)}, f32[8,16,1024]{2,1,0:T(8,128)}, s32[]{:T(128)}, s32[8]{0:T(128)S(1)}, f32[16,1024]{1,0:T(8,128)S(1)}, /*index=5*/f32[8,16,1024]{2,1,0:T(8,128)}, s32[]{:T(128)}) while((s32[]{:T(128)}, f32[8,16,1024]{2,1,0:T(8,128)}, s32[]{:T(128)}, s32[8]{0:T(128)S(1)}, f32[16,1024]{1,0:T(8,128)S(1)}, ...), condition=%wide.region_26.27_spmd, body=%wide.region_25.26_spmd.sunk | while | flops 1441802 | bytes 1638537 | solution.py:66
  388.5 2.3 subtract_select_fusion.38
  391.5 2.3 subtract_select_fusion.38
  394.4 2.3 subtract_select_fusion.38
  397.3 4.8 while.166
  402.2 7.1 %while.165 = (s32[]{:T(128)}, f32[8,16,1024]{2,1,0:T(8,128)S(1)}, s32[]{:T(128)}, s32[8]{0:T(128)S(1)}, f32[16,1024]{1,0:T(8,128)S(1)}, /*index=5*/f32[8,16,1024]{2,1,0:T(8,128)}, s32[]{:T(128)}) while((s32[]{:T(128)}, f32[8,16,1024]{2,1,0:T(8,128)S(1)}, s32[]{:T(128)}, s32[8]{0:T(128)S(1)}, f32[16,1024]{1,0:T(8,128)S(1)}, ...), condition=%wide.region_20.21_spmd, body=%wide.region_19.20_spmd.sunk | while | flops 1441802 | bytes 1638537 | solution.py:66
  409.3 6.8 %while.164 = (s32[]{:T(128)}, f32[8,16,1024]{2,1,0:T(8,128)S(1)}, s32[]{:T(128)}, s32[8]{0:T(128)S(1)}, f32[16,1024]{1,0:T(8,128)S(1)}, /*index=5*/f32[8,16,1024]{2,1,0:T(8,128)}, s32[]{:T(128)}) while((s32[]{:T(128)}, f32[8,16,1024]{2,1,0:T(8,128)S(1)}, s32[]{:T(128)}, s32[8]{0:T(128)S(1)}, f32[16,1024]{1,0:T(8,128)S(1)}, ...), condition=%wide.region_17.18_spmd, body=%wide.region_16.17_spmd.sunk | while | flops 1441802 | bytes 1638537 | solution.py:66
  416.2 17.4 %while.163 = (s32[]{:T(128)}, f32[8,16,1024]{2,1,0:T(8,128)S(1)}, s32[]{:T(128)}, s32[8]{0:T(128)S(1)}, f32[16,1024]{1,0:T(8,128)S(1)}, /*index=5*/f32[8,16,1024]{2,1,0:T(8,128)}, s32[]{:T(128)}) while((s32[]{:T(128)}, f32[8,16,1024]{2,1,0:T(8,128)S(1)}, s32[]{:T(128)}, s32[8]{0:T(128)S(1)}, f32[16,1024]{1,0:T(8,128)S(1)}, ...), condition=%wide.region_14.15_spmd, body=%wide.region_13.14_spmd.sunk | while | flops 1441802 | bytes 1638537 | solution.py:66
  433.6 4.6 while.162
  438.2 17.4 %while.161 = (s32[]{:T(128)}, f32[8,16,1024]{2,1,0:T(8,128)S(1)}, s32[]{:T(128)}, s32[8]{0:T(128)S(1)}, f32[16,1024]{1,0:T(8,128)S(1)}, /*index=5*/f32[8,16,1024]{2,1,0:T(8,128)}, s32[]{:T(128)}) while((s32[]{:T(128)}, f32[8,16,1024]{2,1,0:T(8,128)S(1)}, s32[]{:T(128)}, s32[8]{0:T(128)S(1)}, f32[16,1024]{1,0:T(8,128)S(1)}, ...), condition=%wide.region_8.9_spmd, body=%wide.region_7.8_spmd.sunk | while | flops 1441802 | bytes 1638537 | solution.py:66
  460.2 2.5 collective-permute-start.2
  462.7 4.3 collective-permute-start.3
  467.0 6.3 collective-permute-done.2
  473.3 2.8 collective-permute-done.3
  476.1 3.8 pad_maximum_fusion.3
  480.0 10.6 %fusion.18 = f32[64,16,1024]{2,1,0:T(8,128)S(1)} fusion(f32[64,18,1024]{2,1,0:T(8,128)S(1)} %get-tuple-element.770, f32[64,16,1024]{2,1,0:T(8,128)S(1)} %copy-done.8, f32[64,18,1024]{2,1,0:T(8,128)S(1)} %get-tuple-element.769, f32[64,1,1024]{2,1,0:T(1,128)} %collective-permute-done.3, f32[64,1,1024]{2,1,0:T(1,128)} %copy-done.10, f32[16,1024]{1,0:T(8,128)} %param.46, ...), kind=kLoop, calls=%fused_computation.70 | loop fusion | flops 26214400 | bytes 34209792 | tf_op jit(solution)/shard_map/add | solution.py:70
  492.6 7.5 %while.176 = (s32[]{:T(128)}, f32[8,16,1024]{2,1,0:T(8,128)}, s32[]{:T(128)}, s32[8]{0:T(128)}, f32[16,1024]{1,0:T(8,128)S(1)}, /*index=5*/f32[8,16,1024]{2,1,0:T(8,128)}, s32[]{:T(128)}) while((s32[]{:T(128)}, f32[8,16,1024]{2,1,0:T(8,128)}, s32[]{:T(128)}, s32[8]{0:T(128)}, f32[16,1024]{1,0:T(8,128)S(1)}, ...), condition=%wide.region_45.46_spmd, body=%wide.region_44.45_spmd.sunk | while | flops 1441802 | bytes 1638537 | solution.py:66
  493.8 2.3 subtract_select_fusion.47
  497.3 2.3 subtract_select_fusion.47
  500.1 9.4 %while.175 = (s32[]{:T(128)}, f32[8,16,1024]{2,1,0:T(8,128)}, s32[]{:T(128)}, s32[8]{0:T(128)S(1)}, f32[16,1024]{1,0:T(8,128)S(1)}, /*index=5*/f32[8,16,1024]{2,1,0:T(8,128)}, s32[]{:T(128)}) while((s32[]{:T(128)}, f32[8,16,1024]{2,1,0:T(8,128)}, s32[]{:T(128)}, s32[8]{0:T(128)S(1)}, f32[16,1024]{1,0:T(8,128)S(1)}, ...), condition=%wide.region_43.44_spmd, body=%wide.region_42.43_spmd.sunk | while | flops 1441802 | bytes 1638537 | solution.py:66
  500.8 2.3 subtract_select_fusion.46
  503.7 2.3 subtract_select_fusion.46
  506.6 2.3 subtract_select_fusion.46
  509.6 4.8 while.174
  514.4 6.9 %while.173 = (s32[]{:T(128)}, f32[8,16,1024]{2,1,0:T(8,128)S(1)}, s32[]{:T(128)}, s32[8]{0:T(128)S(1)}, f32[16,1024]{1,0:T(8,128)S(1)}, /*index=5*/f32[8,16,1024]{2,1,0:T(8,128)}, s32[]{:T(128)}) while((s32[]{:T(128)}, f32[8,16,1024]{2,1,0:T(8,128)S(1)}, s32[]{:T(128)}, s32[8]{0:T(128)S(1)}, f32[16,1024]{1,0:T(8,128)S(1)}, ...), condition=%wide.region_39.40_spmd, body=%wide.region_38.39_spmd.sunk | while | flops 1441802 | bytes 1638537 | solution.py:66
  521.4 6.8 %while.172 = (s32[]{:T(128)}, f32[8,16,1024]{2,1,0:T(8,128)S(1)}, s32[]{:T(128)}, s32[8]{0:T(128)S(1)}, f32[16,1024]{1,0:T(8,128)S(1)}, /*index=5*/f32[8,16,1024]{2,1,0:T(8,128)}, s32[]{:T(128)}) while((s32[]{:T(128)}, f32[8,16,1024]{2,1,0:T(8,128)S(1)}, s32[]{:T(128)}, s32[8]{0:T(128)S(1)}, f32[16,1024]{1,0:T(8,128)S(1)}, ...), condition=%wide.region_37.38_spmd, body=%wide.region_36.37_spmd.sunk | while | flops 1441802 | bytes 1638537 | solution.py:66
  528.2 17.4 %while.171 = (s32[]{:T(128)}, f32[8,16,1024]{2,1,0:T(8,128)S(1)}, s32[]{:T(128)}, s32[8]{0:T(128)S(1)}, f32[16,1024]{1,0:T(8,128)S(1)}, /*index=5*/f32[8,16,1024]{2,1,0:T(8,128)}, s32[]{:T(128)}) while((s32[]{:T(128)}, f32[8,16,1024]{2,1,0:T(8,128)S(1)}, s32[]{:T(128)}, s32[8]{0:T(128)S(1)}, f32[16,1024]{1,0:T(8,128)S(1)}, ...), condition=%wide.region_35.36_spmd, body=%wide.region_34.35_spmd.sunk | while | flops 1441802 | bytes 1638537 | solution.py:66
  545.7 4.6 while.170
  550.3 17.4 %while.169 = (s32[]{:T(128)}, f32[8,16,1024]{2,1,0:T(8,128)S(1)}, s32[]{:T(128)}, s32[8]{0:T(128)S(1)}, f32[16,1024]{1,0:T(8,128)S(1)}, /*index=5*/f32[8,16,1024]{2,1,0:T(8,128)}, s32[]{:T(128)}) while((s32[]{:T(128)}, f32[8,16,1024]{2,1,0:T(8,128)S(1)}, s32[]{:T(128)}, s32[8]{0:T(128)S(1)}, f32[16,1024]{1,0:T(8,128)S(1)}, ...), condition=%wide.region_31.32_spmd, body=%wide.region_30.31_spmd.sunk | while | flops 1441802 | bytes 1638537 | solution.py:66
  574.4 5.0 all_to_all.30
  579.4 5.1 all-to-all-start.2
  587.5 45.2 %all-to-all-done.2 = f32[4,16,16384]{2,1,0:T(8,128)} async-done(((f32[4,16,16384]{2,1,0:T(8,128)}), f32[4,16,16384]{2,1,0:T(8,128)}, u32[]{:S(2)}, u32[]{:S(2)}) %all-to-all-start.2) | async-done | bytes 4194336 | tf_op jit(solution)/shard_map/all_to_all | solution.py:141
  632.7 7.7 %gather_fusion.4 = f32[64,16384]{1,0:T(8,128)} fusion(f32[64,16384]{1,0:T(8,128)} %bitcast.19, s32[1024]{0:T(1024)S(1)} %pad_clamp_fusion), kind=kCustom, calls=%fused_computation.4 | custom fusion | bytes 8388864 | tf_op jit(solution)/shard_map/jit(_take)/gather | solution.py:146
  640.4 4.6 copy.27
  645.0 2.4 bitcast_select_fusion
  (279 shorter events, 140.8 us)
Async XLA Ops:
  19.0 5.1 copy-start.1
  19.0 8.7 %copy-start.14 = (s32[1024]{0:T(1024)S(1)}, s32[1024]{0:T(1024)}, u32[]{:S(2)}) copy-start(s32[1024]{0:T(1024)} %param.41) | copy-start | bytes 12292
  19.0 53.2 %all-to-all-start = ((f32[64,4,4096]{2,0,1:T(8,128)}), f32[64,4,4096]{2,0,1:T(8,128)}, u32[]{:S(2)}, u32[]{:S(2)}) async-start(f32[64,4,4096]{2,0,1:T(8,128)} %copy.13), calls=%async_computation | async-start | bytes 8388608 | tf_op jit(solution)/shard_map/all_to_all | solution.py:98
  24.0 203.0 %all-reduce.6.cloned.1.call-start = ((), (), s32[]{:S(2)}) async-start(), calls=%async_computation.3 | async-start | bytes 524288 | tf_op jit(solution)/shard_map/psum | solution.py:112
  27.3 44.8 %copy-start.13 = (s32[4,16,4]{2,1,0:T(8,128)}, s32[4,16,4]{2,1,0:T(8,128)S(1)}, u32[]{:S(2)}) copy-start(s32[4,16,4]{2,1,0:T(8,128)S(1)} %reshape.164) | copy-start | bytes 3076
  91.2 5.7 copy-start.15
  91.2 5.7 copy-start.16
  255.2 53.1 %all-to-all-start.1 = ((f32[4,64,4096]{2,1,0:T(8,128)}), f32[4,64,4096]{2,1,0:T(8,128)}, u32[]{:S(2)}, u32[]{:S(2)}) async-start(f32[4,64,4096]{2,1,0:T(8,128)} %pad_maximum_fusion.10), calls=%async_computation.1 | async-start | bytes 8388608 | tf_op jit(solution)/shard_map/all_to_all | solution.py:131
  315.2 5.9 copy-start.11
  324.6 32.6 %collective-permute-start = (f32[65,1,1024]{2,1,0:T(1,128)}, f32[65,1,1024]{2,1,0:T(1,128)S(1)}, u32[]{:S(2)}, u32[]{:S(2)}) collective-permute-start(f32[65,1,1024]{2,1,0:T(1,128)} %get-tuple-element.771), channel_id=1, source_target_pairs={{0,1},{1,2},{2,3},{3,4},{4,5},{5,6},{6,7},{8,9},{9,10},{10,11},{11... | collective-permute-start | bytes 798728 | tf_op jit(solution)/shard_map/ppermute | solution.py:19
  328.0 29.2 %collective-permute-start.1 = (f32[65,1,1024]{2,1,0:T(1,128)}, f32[65,1,1024]{2,1,0:T(1,128)}, u32[]{:S(2)}, u32[]{:S(2)}) collective-permute-start(f32[65,1,1024]{2,1,0:T(1,128)} %get-tuple-element.772), channel_id=1, source_target_pairs={{1,0},{2,1},{3,2},{4,3},{5,4},{6,5},{7,6},{9,8},{10,9},{11,10},{12... | collective-permute-start | bytes 798728 | tf_op jit(solution)/shard_map/ppermute | solution.py:20
  357.2 2.3 copy-start.2
  357.2 6.1 copy-start.9
  359.5 3.8 copy-start.12
  359.5 3.8 copy-start
  380.3 7.6 %copy-start.27 = (s32[8]{0:T(128)S(1)}, s32[8]{0:T(128)}, u32[]{:S(2)}) copy-start(s32[8]{0:T(128)} %get-tuple-element.1718) | copy-start | bytes 100
  387.9 9.4 %copy-start.25 = (s32[8]{0:T(128)S(1)}, s32[8]{0:T(128)}, u32[]{:S(2)}) copy-start(s32[8]{0:T(128)} %get-tuple-element.1697) | copy-start | bytes 100
  397.3 4.9 copy-start.23
  402.1 7.2 %copy-start.21 = (s32[8]{0:T(128)S(1)}, s32[8]{0:T(128)}, u32[]{:S(2)}) copy-start(s32[8]{0:T(128)} %get-tuple-element.1655) | copy-start | bytes 100
  409.3 6.9 %copy-start.19 = (s32[8]{0:T(128)S(1)}, s32[8]{0:T(128)}, u32[]{:S(2)}) copy-start(s32[8]{0:T(128)} %get-tuple-element.1634) | copy-start | bytes 100
  416.2 17.5 %copy-start.17 = (s32[8]{0:T(128)S(1)}, s32[8]{0:T(128)}, u32[]{:S(2)}) copy-start(s32[8]{0:T(128)} %get-tuple-element.1613) | copy-start | bytes 100
  455.6 1.0 copy-start.3
  455.6 1.2 copy-start.5
  456.9 2.0 copy-start.7
  460.2 13.1 %collective-permute-start.2 = (f32[64,1,1024]{2,1,0:T(1,128)}, f32[64,1,1024]{2,1,0:T(1,128)S(1)}, u32[]{:S(2)}, u32[]{:S(2)}) collective-permute-start(f32[64,1,1024]{2,1,0:T(1,128)} %get-tuple-element.781), channel_id=1, source_target_pairs={{0,1},{1,2},{2,3},{3,4},{4,5},{5,6},{6,7},{8,9},{9,10},{10,11},{11... | collective-permute-start | bytes 786440 | tf_op jit(solution)/shard_map/ppermute | solution.py:19
  462.7 13.4 %collective-permute-start.3 = (f32[64,1,1024]{2,1,0:T(1,128)}, f32[64,1,1024]{2,1,0:T(1,128)}, u32[]{:S(2)}, u32[]{:S(2)}) collective-permute-start(f32[64,1,1024]{2,1,0:T(1,128)} %get-tuple-element.782), channel_id=1, source_target_pairs={{1,0},{2,1},{3,2},{4,3},{5,4},{6,5},{7,6},{9,8},{10,9},{11,10},{12... | collective-permute-start | bytes 786440 | tf_op jit(solution)/shard_map/ppermute | solution.py:20
  467.0 13.0 %copy-start.8 = (f32[64,16,1024]{2,1,0:T(8,128)S(1)}, f32[64,16,1024]{2,1,0:T(8,128)}, u32[]{:S(2)}) copy-start(f32[64,16,1024]{2,1,0:T(8,128)} %copy-done.7) | copy-start | bytes 12582916
  473.3 6.6 %copy-start.10 = (f32[64,1,1024]{2,1,0:T(1,128)}, f32[64,1,1024]{2,1,0:T(1,128)S(1)}, u32[]{:S(2)}) copy-start(f32[64,1,1024]{2,1,0:T(1,128)S(1)} %collective-permute-done.2) | copy-start | bytes 786436
  492.6 7.6 %copy-start.28 = (s32[8]{0:T(128)S(1)}, s32[8]{0:T(128)}, u32[]{:S(2)}) copy-start(s32[8]{0:T(128)} %get-tuple-element.1718) | copy-start | bytes 100
  500.1 9.4 %copy-start.26 = (s32[8]{0:T(128)S(1)}, s32[8]{0:T(128)}, u32[]{:S(2)}) copy-start(s32[8]{0:T(128)} %get-tuple-element.1697) | copy-start | bytes 100
  509.5 4.9 copy-start.24
  514.4 7.0 %copy-start.22 = (s32[8]{0:T(128)S(1)}, s32[8]{0:T(128)}, u32[]{:S(2)}) copy-start(s32[8]{0:T(128)} %get-tuple-element.1655) | copy-start | bytes 100
  521.4 6.9 %copy-start.20 = (s32[8]{0:T(128)S(1)}, s32[8]{0:T(128)}, u32[]{:S(2)}) copy-start(s32[8]{0:T(128)} %get-tuple-element.1634) | copy-start | bytes 100
  528.2 17.5 %copy-start.18 = (s32[8]{0:T(128)S(1)}, s32[8]{0:T(128)}, u32[]{:S(2)}) copy-start(s32[8]{0:T(128)} %get-tuple-element.1613) | copy-start | bytes 100
  567.7 5.1 copy-start.4
  567.7 5.9 copy-start.6
  579.4 53.3 %all-to-all-start.2 = ((f32[4,16,16384]{2,1,0:T(8,128)}), f32[4,16,16384]{2,1,0:T(8,128)}, u32[]{:S(2)}, u32[]{:S(2)}) async-start(f32[4,16,16384]{2,1,0:T(8,128)} %all_to_all.30), calls=%async_computation.2 | async-start | bytes 8388608 | tf_op jit(solution)/shard_map/all_to_all | solution.py:141
Sparse Core Ops, SparseCore 0:
  100.1 126.7 all-reduce.5
